TPU v7x, 32 devices: a whole 2x2x4 slice. The times are simulated.
32 devices in a mesh: seq: 16 (over z, x, core), chan: 2 (over y).
Axes of the slice: x: 2, y: 2, z: 4, core: 2. Of those that a mesh axis runs over, the one named last changes fastest.
Arguments:
- step_size: bfloat16 [2, 5120, 2048], P(None, ('chan', 'seq')), as said below
- inputs: bfloat16 [2, 5120, 2048], P(None, ('chan', 'seq')), may hold values from -6 to 6
- gate_input: bfloat16 [2, 5120, 2048], P(None, ('chan', 'seq')), may hold values from -6 to 6
- decay_rate: float32 [5120], P('chan'), as said below
- norm_gain: float32 [5120], P('chan'), may hold values from 0.1 to 1.9
- resets: int32 [2, 8], replicated, may hold values from 1 to 2047
Outputs:
- normed: bfloat16 [2, 5120, 2048], P(None, 'chan', 'seq')
Inputs may be any that keep to these rules, and one draw needn't show every extreme that they name: `step_size`: positive step sizes. `decay_rate`: positive rates. `resets`: positions within the sequence; several may coincide.
All inputs are finite; a program needn't handle non-finite values.
Results may differ from a plain program's by a relative error of at most 0.001.
Values may be sent and summed in bfloat16 or wider, within the bound.
A program may use at most 64 MiB of HBM per device.

v0:
```python
import math
import jax
import jax.numpy as jnp
from jax import lax
from jax.sharding import PartitionSpec as P

FEATURE_WIDTH = 5120


def compose(earlier, later):
    return (earlier[0] * later[0], later[0] * earlier[1] + later[1])


def coefficients(steps, values, rates):
    scaled = steps.astype(jnp.float32) * rates[None, :, None]
    drive = jnp.sqrt(-jnp.expm1(-2.0 * scaled)) * values.astype(jnp.float32)
    return (scaled, drive)


def marks_for(resets, places):
    return jnp.any(resets[:, :, None] == places[None, None, :], axis=1)


def local_scan(scaled, drive, marks):
    rows, chans, length = scaled.shape
    places = jnp.arange(length, dtype=jnp.int32)
    upper = (places[:, None] <= places[None, :]).astype(jnp.float32)
    cumul = jnp.einsum("rck,ku->rcu", scaled, upper, precision=lax.Precision.HIGHEST)
    counts = jnp.dot(marks.astype(jnp.float32), upper, precision=lax.Precision.HIGHEST)
    linked = (counts[:, :, None] == counts[:, None, :]) & (places[:, None] >= places[None, :])[None]
    group = math.gcd(chans, 64)

    def one_group(pieces):
        cumul_part, drive_part = pieces
        spread = cumul_part[:, :, :, None] - cumul_part[:, :, None, :]
        weight = jnp.where(linked[:, None], jnp.exp(-jnp.maximum(spread, 0.0)), jnp.float32(0.0))
        return jnp.einsum("rctj,rcj->rct", weight, drive_part, precision=lax.Precision.HIGHEST)

    def split_groups(array):
        return jnp.moveaxis(array.reshape(rows, chans // group, group, length), 1, 0)

    results = lax.map(one_group, (split_groups(cumul), split_groups(drive)))
    local_state = jnp.moveaxis(results, 0, 1).reshape(rows, chans, length)
    running = jnp.where(counts[:, None, :] == 0.0, jnp.exp(-cumul), jnp.float32(0.0))
    return (running, local_state)


def finish(gated, norm_gain):
    squares = jnp.sum(gated * gated, axis=1)
    total = lax.psum(squares, "chan")
    mean_square = total / jnp.float32(FEATURE_WIDTH)
    scale_rows = lax.rsqrt(mean_square + 1e-05)
    return (gated * scale_rows[:, None, :] * norm_gain[None, :, None]).astype(jnp.bfloat16)


def per_device(step_size, inputs, gate_input, decay_rate, norm_gain, resets):
    position = lax.axis_index("seq")
    batch, width, length = step_size.shape
    rates = lax.dynamic_slice_in_dim(decay_rate, position * width, width)
    places = jnp.arange(length, dtype=jnp.int32)
    scaled, drive = coefficients(step_size, inputs, rates)
    marks = marks_for(resets, places)
    piece = math.gcd(length, 128)
    count_blocks = length // piece

    def to_blocks(array):
        moved = jnp.moveaxis(array.reshape(batch, width, count_blocks, piece), 2, 1)
        return moved.reshape(batch * count_blocks, width, piece)

    running, local_state = local_scan(
        to_blocks(scaled), to_blocks(drive), marks.reshape(batch * count_blocks, piece)
    )
    total_decay = running[:, :, -1].reshape(batch, count_blocks, width)
    total_state = local_state[:, :, -1].reshape(batch, count_blocks, width)
    prefix = lax.associative_scan(compose, (total_decay, total_state), axis=1)
    incoming = jnp.concatenate(
        [jnp.zeros((batch, 1, width), jnp.float32), prefix[1][:, :-1]], axis=1
    )
    blocked = local_state + running * incoming.reshape(batch * count_blocks, width)[:, :, None]
    state = jnp.moveaxis(blocked.reshape(batch, count_blocks, width, piece), 1, 2).reshape(
        batch, width, length
    )
    local_gated = state * jax.nn.silu(gate_input.astype(jnp.float32))
    gated = lax.all_to_all(local_gated, "seq", split_axis=2, concat_axis=1, tiled=True)
    return finish(gated, norm_gain)


def solution(mesh):
    in_specs = (
        P(None, ("chan", "seq"), None),
        P(None, ("chan", "seq"), None),
        P(None, ("chan", "seq"), None),
        P("chan"),
        P("chan"),
        P(),
    )
    out_specs = P(None, "chan", "seq")
    return jax.shard_map(
        per_device, mesh=mesh, in_specs=in_specs, out_specs=out_specs, check_vma=False
    )
```

profile of v0, /device:TPU:0, one launch (start us, length us, event | category | flops | bytes accessed | tf_op | source)
XLA Modules:
  0.0 738.9 jit_solution(2449741942070967262)
XLA Ops:
  0.0 0.8 dynamic_slice.10
  0.8 5.1 convert_multiply_fusion.1
  5.9 0.5 copy.63
  6.4 0.2 bitcast_bitcast_fusion.1
  6.6 0.8 copy.51
  7.4 0.1 fusion.19
  7.5 0.1 broadcast_compare_fusion
  7.7 2.9 exponential_select_fusion
  10.6 0.2 copy.68
  10.8 1.5 copy-done.2
  12.3 0.5 copy.64
  12.8 0.2 bitcast_bitcast_fusion
  13.0 2.3 copy.53
  15.3 581.5 %while.11 = (s32[]{:T(128)}, f32[5,32,32,128]{3,2,1,0:T(8,128)}, f32[5,32,32,128]{3,2,1,0:T(8,128)S(1)}, f32[5,32,32,128]{3,2,0,1:T(8,128)}, f32[32,128]{1,0:T(8...) while((s32[]{:T(128)}, f32[5,32,32,128]{3,2,1,0:T(8,128)}, f32[5,32,32,128]{3,2,1,0:T(8,128)S(1)}, ...), condition=%wide.region_2.3_spmd.clone, body=%wide.region_1.2_spmd.clone.sunk | while | flops 269484032 | bytes 5800533 | solution.py:42
  29.8 1.1 constant_dynamic-slice_fusion.2
  30.9 0.7 compare_and_fusion.2
  31.6 110.7 %fusion.44 = f32[32,32,1,128]{3,2,1,0:T(1,128)S(1)} fusion(f32[32,32,128,1]{2,3,1,0:T(1,128)S(1)} %bitcast.83, f32[32,32,128]{2,1,0:T(8,128)S(1)} %dynamic-slice_bitcast_fusion.2, pred[32,128,128]{2,1,0:T(8,128)(4,1)S(1)} %compare_and_fusion.2), kind=kOutput, calls=%fused_computation.1.clone.2 | convolution fusion | flops 268435456 | bytes 2097152 | tf_op jit(solution)/shard_map/while/body/eval_jaxpr/rctj,rcj->rct/dot_general | solution.py:37
  142.3 0.9 constant_dynamic-update-slice_fusion.2
  143.2 1.1 constant_dynamic-slice_fusion.2
  144.3 0.7 compare_and_fusion.2
  145.0 110.7 %fusion.44 = f32[32,32,1,128]{3,2,1,0:T(1,128)S(1)} fusion(f32[32,32,128,1]{2,3,1,0:T(1,128)S(1)} %bitcast.83, f32[32,32,128]{2,1,0:T(8,128)S(1)} %dynamic-slice_bitcast_fusion.2, pred[32,128,128]{2,1,0:T(8,128)(4,1)S(1)} %compare_and_fusion.2), kind=kOutput, calls=%fused_computation.1.clone.2 | convolution fusion | flops 268435456 | bytes 2097152 | tf_op jit(solution)/shard_map/while/body/eval_jaxpr/rctj,rcj->rct/dot_general | solution.py:37
  255.7 0.9 constant_dynamic-update-slice_fusion.2
  256.6 1.1 constant_dynamic-slice_fusion.2
  257.7 0.7 compare_and_fusion.2
  258.5 110.7 %fusion.44 = f32[32,32,1,128]{3,2,1,0:T(1,128)S(1)} fusion(f32[32,32,128,1]{2,3,1,0:T(1,128)S(1)} %bitcast.83, f32[32,32,128]{2,1,0:T(8,128)S(1)} %dynamic-slice_bitcast_fusion.2, pred[32,128,128]{2,1,0:T(8,128)(4,1)S(1)} %compare_and_fusion.2), kind=kOutput, calls=%fused_computation.1.clone.2 | convolution fusion | flops 268435456 | bytes 2097152 | tf_op jit(solution)/shard_map/while/body/eval_jaxpr/rctj,rcj->rct/dot_general | solution.py:37
  369.2 0.9 constant_dynamic-update-slice_fusion.2
  370.0 1.1 constant_dynamic-slice_fusion.2
  371.1 0.7 compare_and_fusion.2
  371.9 110.7 %fusion.44 = f32[32,32,1,128]{3,2,1,0:T(1,128)S(1)} fusion(f32[32,32,128,1]{2,3,1,0:T(1,128)S(1)} %bitcast.83, f32[32,32,128]{2,1,0:T(8,128)S(1)} %dynamic-slice_bitcast_fusion.2, pred[32,128,128]{2,1,0:T(8,128)(4,1)S(1)} %compare_and_fusion.2), kind=kOutput, calls=%fused_computation.1.clone.2 | convolution fusion | flops 268435456 | bytes 2097152 | tf_op jit(solution)/shard_map/while/body/eval_jaxpr/rctj,rcj->rct/dot_general | solution.py:37
  482.6 0.9 constant_dynamic-update-slice_fusion.2
  483.4 1.1 constant_dynamic-slice_fusion.2
  484.6 0.7 compare_and_fusion.2
  485.3 110.7 %fusion.44 = f32[32,32,1,128]{3,2,1,0:T(1,128)S(1)} fusion(f32[32,32,128,1]{2,3,1,0:T(1,128)S(1)} %bitcast.83, f32[32,32,128]{2,1,0:T(8,128)S(1)} %dynamic-slice_bitcast_fusion.2, pred[32,128,128]{2,1,0:T(8,128)(4,1)S(1)} %compare_and_fusion.2), kind=kOutput, calls=%fused_computation.1.clone.2 | convolution fusion | flops 268435456 | bytes 2097152 | tf_op jit(solution)/shard_map/while/body/eval_jaxpr/rctj,rcj->rct/dot_general | solution.py:37
  596.0 0.8 constant_dynamic-update-slice_fusion.2
  596.8 2.0 copy.55
  598.8 1.5 copy-done.1
  600.3 1.9 slice_reduce_fusion.1
  602.2 1.9 slice_reduce_fusion
  604.8 2.2 multiply_add_fusion
  607.0 3.0 copy.67
  610.0 2.6 reshape.57
  612.6 3.5 fusion.16
  616.1 6.8 copy.57
  622.9 99.6 %all_to_all.18 = f32[2,160,2048]{1,0,2:T(2,128)} all-to-all(f32[2,160,2048]{1,0,2:T(2,128)} %copy.57), channel_id=1, replica_groups=mesh['seq'=16,'chan'=2] {'seq'}, dimensions={2} | all-to-all | bytes 5242880 | tf_op jit(solution)/shard_map/all_to_all | solution.py:84
  722.5 5.3 copy.58
  727.8 4.2 multiply_reduce_fusion
  732.0 5.0 psum.7
  737.0 1.5 fusion.18
  (57 shorter events, 1.0 us)
Async XLA Ops:
  6.6 0.8 copy-start.4
  10.6 1.7 copy-start.2
  598.8 1.5 copy-start.1
  598.8 3.4 copy-start
  727.8 9.2 %copy-start.3 = (f32[2560]{0:T(1024)S(1)}, f32[2560]{0:T(1024)}, u32[]{:S(2)}) copy-start(f32[2560]{0:T(1024)} %param.12) | copy-start | bytes 30724
where the time goes:
time: 745 us; the launch traced here: 739 us
  matrix products  556 us (75%)
  blocking collectives  105 us (14%)
  local copies, waits for them, and re-layouts  42.4 us (6%)
  other arithmetic  20.3 us (3%)
  loops' own time  14.5 us (2%)
    dot_general x5, matrix products, one_group(): jnp.einsum('rctj,rcj->rct', weight, drive_part, precision=lax.Precision.H...  553 us
    all_to_all x1, blocking collectives, per_device(): lax.all_to_all(local_gated, 'seq', split_axis=2, concat_axis=1, tiled=True)  99.6 us

commit v1 on v0

--- a/solution.py
+++ b/solution.py
@@ -81,7 +81,9 @@
         batch, width, length
     )
     local_gated = state * jax.nn.silu(gate_input.astype(jnp.float32))
-    gated = lax.all_to_all(local_gated, "seq", split_axis=2, concat_axis=1, tiled=True)
+    shards = jnp.split(local_gated, lax.axis_size("seq"), axis=2)
+    incoming_2 = lax.all_to_all(jnp.stack(shards), "seq", 0, 0)
+    gated = jnp.concatenate(incoming_2, axis=1)
     return finish(gated, norm_gain)
 
 

time: 745 us -> 667 us (0.90)
  blocking collectives: 105 us -> 70.5 us
  local copies, waits for them, and re-layouts: 42.4 us -> 25.2 us
  loops' own time: 14.5 us -> 0.1 us
    all_to_all x1, blocking collectives: 99.6 us -> 65.6 us  [per_device(): incoming_2 = lax.all_to_all(jnp.stack(shards), 'seq', 0, 0)]
    another operation x1, loops' own time: 14.5 us -> 0.1 us  [local_scan(): results = lax.map(one_group, (split_groups(cumul), split_groups(drive)))]
where the time goes in v1:
time: 667 us; the launch traced here: 666 us
  matrix products  556 us (83%)
  blocking collectives  70.5 us (11%)
  local copies, waits for them, and re-layouts  25.2 us (4%)
  other arithmetic  13.7 us (2%)
    dot_general x5, matrix products, one_group(): jnp.einsum('rctj,rcj->rct', weight, drive_part, precision=lax.Precision.H...  553 us
    all_to_all x1, blocking collectives, per_device(): incoming_2 = lax.all_to_all(jnp.stack(shards), 'seq', 0, 0)  65.6 us

profile of v1, /device:TPU:0, one launch (start us, length us, event | category | flops | bytes accessed | tf_op | source)
XLA Modules:
  0.0 666.4 jit_solution(189833215169826504)
XLA Ops:
  0.0 0.8 dynamic_slice.10
  0.8 5.1 convert_multiply_fusion.1
  5.9 0.5 copy.36
  6.4 0.2 bitcast_bitcast_fusion.1
  6.6 0.0 copy-start.5
  6.6 0.8 copy.25
  7.4 0.1 fusion.35
  7.5 0.1 broadcast_compare_fusion
  7.7 2.9 exponential_select_fusion
  10.6 0.2 copy.40
  10.8 1.5 copy-done.2
  12.3 0.5 copy.37
  12.8 0.2 bitcast_bitcast_fusion
  13.0 2.3 copy.27
  15.3 567.1 %while.11 = (s32[]{:T(128)}, f32[5,32,32,128]{3,2,1,0:T(8,128)}, f32[5,32,32,128]{3,2,1,0:T(8,128)S(1)}, f32[5,32,32,128]{3,2,0,1:T(8,128)}, f32[32,128]{1,0:T(8...) while((s32[]{:T(128)}, f32[5,32,32,128]{3,2,1,0:T(8,128)}, f32[5,32,32,128]{3,2,1,0:T(8,128)S(1)}, ...), condition=%wide.region_2.3_spmd.clone, body=%wide.region_1.2_spmd.clone.sunk | while | flops 269484032 | bytes 5800533 | solution.py:42
  15.3 1.1 constant_dynamic-slice_fusion.2
  16.5 0.7 compare_and_fusion.2
  17.2 110.7 %fusion.60 = f32[32,32,1,128]{3,2,1,0:T(1,128)S(1)} fusion(f32[32,32,128,1]{2,3,1,0:T(1,128)S(1)} %bitcast.145, f32[32,32,128]{2,1,0:T(8,128)S(1)} %dynamic-slice_bitcast_fusion.2, pred[32,128,128]{2,1,0:T(8,128)(4,1)S(1)} %compare_and_fusion.2), kind=kOutput, calls=%fused_computation.1.clone.2 | convolution fusion | flops 268435456 | bytes 2097152 | tf_op jit(solution)/shard_map/while/body/eval_jaxpr/rctj,rcj->rct/dot_general | solution.py:37
  127.9 0.9 constant_dynamic-update-slice_fusion.2
  128.7 1.1 constant_dynamic-slice_fusion.2
  129.9 0.7 compare_and_fusion.2
  130.6 110.7 %fusion.60 = f32[32,32,1,128]{3,2,1,0:T(1,128)S(1)} fusion(f32[32,32,128,1]{2,3,1,0:T(1,128)S(1)} %bitcast.145, f32[32,32,128]{2,1,0:T(8,128)S(1)} %dynamic-slice_bitcast_fusion.2, pred[32,128,128]{2,1,0:T(8,128)(4,1)S(1)} %compare_and_fusion.2), kind=kOutput, calls=%fused_computation.1.clone.2 | convolution fusion | flops 268435456 | bytes 2097152 | tf_op jit(solution)/shard_map/while/body/eval_jaxpr/rctj,rcj->rct/dot_general | solution.py:37
  241.3 0.9 constant_dynamic-update-slice_fusion.2
  242.2 1.1 constant_dynamic-slice_fusion.2
  243.3 0.7 compare_and_fusion.2
  244.0 110.7 %fusion.60 = f32[32,32,1,128]{3,2,1,0:T(1,128)S(1)} fusion(f32[32,32,128,1]{2,3,1,0:T(1,128)S(1)} %bitcast.145, f32[32,32,128]{2,1,0:T(8,128)S(1)} %dynamic-slice_bitcast_fusion.2, pred[32,128,128]{2,1,0:T(8,128)(4,1)S(1)} %compare_and_fusion.2), kind=kOutput, calls=%fused_computation.1.clone.2 | convolution fusion | flops 268435456 | bytes 2097152 | tf_op jit(solution)/shard_map/while/body/eval_jaxpr/rctj,rcj->rct/dot_general | solution.py:37
  354.7 0.9 constant_dynamic-update-slice_fusion.2
  355.6 1.1 constant_dynamic-slice_fusion.2
  356.7 0.7 compare_and_fusion.2
  357.4 110.7 %fusion.60 = f32[32,32,1,128]{3,2,1,0:T(1,128)S(1)} fusion(f32[32,32,128,1]{2,3,1,0:T(1,128)S(1)} %bitcast.145, f32[32,32,128]{2,1,0:T(8,128)S(1)} %dynamic-slice_bitcast_fusion.2, pred[32,128,128]{2,1,0:T(8,128)(4,1)S(1)} %compare_and_fusion.2), kind=kOutput, calls=%fused_computation.1.clone.2 | convolution fusion | flops 268435456 | bytes 2097152 | tf_op jit(solution)/shard_map/while/body/eval_jaxpr/rctj,rcj->rct/dot_general | solution.py:37
  468.1 0.9 constant_dynamic-update-slice_fusion.2
  469.0 1.1 constant_dynamic-slice_fusion.2
  470.1 0.7 compare_and_fusion.2
  470.9 110.7 %fusion.60 = f32[32,32,1,128]{3,2,1,0:T(1,128)S(1)} fusion(f32[32,32,128,1]{2,3,1,0:T(1,128)S(1)} %bitcast.145, f32[32,32,128]{2,1,0:T(8,128)S(1)} %dynamic-slice_bitcast_fusion.2, pred[32,128,128]{2,1,0:T(8,128)(4,1)S(1)} %compare_and_fusion.2), kind=kOutput, calls=%fused_computation.1.clone.2 | convolution fusion | flops 268435456 | bytes 2097152 | tf_op jit(solution)/shard_map/while/body/eval_jaxpr/rctj,rcj->rct/dot_general | solution.py:37
  581.5 0.8 constant_dynamic-update-slice_fusion.2
  582.4 2.0 copy.29
  584.4 1.5 copy-done.1
  585.9 1.9 slice_reduce_fusion.1
  587.8 1.9 slice_reduce_fusion
  590.4 0.0 copy-start.3
  590.4 2.3 multiply_add_fusion
  592.7 0.7 fusion.16
  593.9 65.6 %all_to_all.5 = f32[16,2,160,128]{3,2,1,0:T(8,128)S(1)} all-to-all(f32[16,2,160,128]{3,2,1,0:T(8,128)S(1)} %fusion.19), channel_id=1, replica_groups=mesh['seq'=16,'chan'=2] {'seq'}, dimensions={0} | all-to-all | bytes 5242880 | tf_op jit(solution)/shard_map/all_to_all | solution.py:85
  659.4 0.2 copy.31
  659.6 0.0 copy-start.4
  659.6 0.4 multiply_reduce_fusion
  660.0 5.0 psum.7
  665.0 1.5 fusion.18
  (71 shorter events, 1.3 us)
Async XLA Ops:
  6.6 0.8 copy-start.5
  10.6 1.7 copy-start.2
  584.4 1.5 copy-start.1
  584.4 3.4 copy-start
  590.4 2.3 copy-start.3
  659.6 5.3 copy-start.4
